TPU v7x, 32 devices: a whole 2x2x4 slice. The times are simulated.
32 devices in a mesh: seq: 4 (over z), head: 4 (over y, x), batch: 2 (over core).
Axes of the slice: x: 2, y: 2, z: 4, core: 2. Of those that a mesh axis runs over, the one named last changes fastest.
Arguments:
- tokens: bfloat16 [4096, 2560], P(('batch', 'seq'), 'head'), parts along dimension 0, may hold values from -6 to 6
- resets: int32 [4096], P(('batch', 'seq')), parts along dimension 0, may hold values 0 or 1
- w_x: bfloat16 [2560, 5120], P(None, 'head'), may hold values from -0.125 to 0.125
- w_z: bfloat16 [2560, 5120], P(None, 'head'), may hold values from -0.125 to 0.125
- w_bc: bfloat16 [2560, 256], replicated, may hold values from -0.125 to 0.125
- w_dt: bfloat16 [2560, 80], P(None, 'head'), may hold values from -0.125 to 0.125
- dt_bias: float32 [80], P('head'), may hold values from -2 to 1
- decay_rate: float32 [80], P('head'), may hold values from 0.00024414062 to 0.08
- d_skip: float32 [80], P('head'), may hold values from 0.5 to 1.5
- norm_gain: float32 [5120], P('head'), may hold values from 0.5 to 1.5
- w_out: bfloat16 [5120, 2560], P('head'), may hold values from -0.078125 to 0.078125
Outputs:
- mixed: bfloat16 [4096, 2560], P(('batch', 'seq'), 'head'), parts along dimension 0
There are 2 independent parts, one for each index of `batch`. A program takes and returns all parts, laid end to end along the dimension named above; an argument that names none is the same for every part. Nothing has to cross between parts.
All inputs are finite; a program needn't handle non-finite values. No bound on the sum of `resets` on one device may be relied on, other than what follows from the above.
Results may differ from a plain program's by a relative error of at most 0.013.
Values may be sent and summed in bfloat16 or wider, within the bound.
A program may use at most 128 MiB of HBM per device.

v0:
```python
import functools

import jax
import jax.numpy as jnp
from jax import lax
from jax.experimental import pallas as pl
from jax.experimental.pallas import tpu as pltpu
from jax.sharding import PartitionSpec as P

HEADDIM = 64
NSTATE = 128
GROUP = 256
LANES = 128
F32 = jnp.float32
BF16 = jnp.bfloat16
MESH = pl.DeviceIdType.MESH
VMEM = pl.BlockSpec(memory_space=pltpu.VMEM)
SMEM = pl.BlockSpec(memory_space=pltpu.SMEM)
ANY = pl.BlockSpec(memory_space=pl.ANY)
EPS = 1e-05


def peers():
    me = lax.axis_index("head")
    across = me + 1 - 2 * lax.rem(me, 2)
    along = lax.rem(me + 2, 4)
    corner = lax.rem(across + 2, 4)
    return me, across, along, corner


def remote(axis, to, src, dst, send, recv):
    return pltpu.make_async_remote_copy(
        src_ref=src, dst_ref=dst, send_sem=send, recv_sem=recv, device_id={axis: to}, device_id_type=MESH
    )


def silu(v):
    return v / (1.0 + jnp.exp(-v))


class Scratch:
    def __init__(self, names, refs):
        for name, ref in zip(names, refs):
            setattr(self, name, ref)


def dot(a, b):
    return jnp.dot(a, b, preferred_element_type=F32)


def dot_nt(a, b, precision=None):
    return lax.dot_general(a, b, (((1,), (1,)), ((), ())), preferred_element_type=F32, precision=precision)


def kernel(chain, total, names, tok, resets, w_x, w_z, w_bc, w_dt, bias, rate, skip, gain, w_out, out, *refs):
    r = Scratch(names, refs)
    me, across, along, corner = peers()
    pos = lax.axis_index("seq")
    upper, lower = lax.rem(pos + 1, chain), lax.rem(pos + chain - 1, chain)
    rows, depth = tok.shape
    width = w_x.shape[1]
    heads = w_dt.shape[0]
    blocks, pairs, per = rows // GROUP, width // LANES, LANES // HEADDIM
    half = GROUP // 2
    owners = (me, across, along, corner)

    def span_of(owner):
        return pl.ds(pl.multiple_of(owner * depth, LANES), depth)

    def rows_of(b):
        return pl.ds(b * GROUP, GROUP)

    def cols_of(j):
        return pl.ds(pl.multiple_of(j * LANES, LANES), LANES)

    loads = [
        (
            pltpu.make_async_copy(w_x.at[span_of(owner)], r.vx.at[k], r.load.at[3 * k]),
            pltpu.make_async_copy(w_z.at[span_of(owner)], r.vz.at[k], r.load.at[3 * k + 1]),
            pltpu.make_async_copy(w_bc.at[span_of(owner)], r.vb.at[k], r.load.at[3 * k + 2]),
        )
        for k, owner in enumerate(owners)
    ]
    order = (corner, across, along, me)
    out_loads = [
        pltpu.make_async_copy(w_out.at[:, span_of(owner)], r.vw.at[k], r.load_out.at[k])
        for k, owner in enumerate(order)
    ]
    for k in (0, 1):
        for copy in loads[k]:
            copy.start()

    barrier = pltpu.get_barrier_semaphore()
    for other in (across, along, corner):
        pl.semaphore_signal(barrier, inc=1, device_id={"head": other}, device_id_type=MESH)
    for other in (upper, lower):
        pl.semaphore_signal(barrier, inc=1, device_id={"seq": other}, device_id_type=MESH)
    pl.semaphore_wait(barrier, 5)

    gathers = []
    for b in range(blocks):
        lo, hi = pl.ds(b * GROUP, half), pl.ds(b * GROUP + half, half)
        plan = (
            (across, tok.at[lo], r.got.at[0, lo]),
            (along, tok.at[hi], r.got.at[1, hi]),
            (across, tok.at[hi], r.got.at[0, hi]),
            (along, tok.at[lo], r.got.at[1, lo]),
            (along, r.got.at[0, lo], r.got.at[2, lo]),
            (across, r.got.at[1, hi], r.got.at[2, hi]),
        )
        gathers.append([
            remote("head", to, src, dst, r.g_send.at[6 * b + i], r.g_recv.at[6 * b + i])
            for i, (to, src, dst) in enumerate(plan)
        ])
    for copy in gathers[0][:4]:
        copy.start()

    wide = 256

    def accumulate(b, k):
        if b == 0:
            for copy in loads[k]:
                copy.wait()
            if k == 0:
                for later in (2, 3):
                    for copy in loads[later]:
                        copy.start()
            if k == 3:
                for copy in out_loads:
                    copy.start()
        rs = rows_of(b)
        block = tok if k == 0 else r.got.at[k - 1]

        def tile(i, _):
            cols = pl.ds(pl.multiple_of(i * wide, wide), wide)
            x = block[rs, :]
            v, z = dot(x, r.vx[k, :, cols]), dot(x, r.vz[k, :, cols])
            if k:
                v, z = v + r.acc_x[:, cols], z + r.acc_z[:, cols]
            if k == 3:
                r.inner[rs, cols] = silu(v).astype(BF16)
                r.gating[rs, cols] = z.astype(BF16)
            else:
                r.acc_x[:, cols] = v
                r.acc_z[:, cols] = z
            return 0

        lax.fori_loop(0, width // wide, tile, 0)
        m = dot(block[rs, :], r.vb[k])
        s = dot_nt(block[rs, :], w_dt[:, span_of(owners[k])])
        if k:
            m, s = m + r.acc_m[...], s + r.acc_s[...]
        if k == 3:
            r.mapped[rs, :] = silu(m).astype(BF16)
            v = s + bias[...]
            r.step[...] = jnp.zeros_like(r.step)
            r.step[:, :heads] = jnp.maximum(v, 0.0) + jnp.log1p(jnp.exp(-jnp.abs(v)))
        else:
            r.acc_m[...] = m
            r.acc_s[...] = s

    def relay(b):
        gathers[b][0].wait_recv()
        gathers[b][4].start()
        gathers[b][1].wait_recv()
        gathers[b][5].start()
        if b + 1 < blocks:
            for copy in gathers[b + 1][:4]:
                copy.start()

    def project(b):
        gathers[b][2].wait_recv()
        accumulate(b, 1)
        gathers[b][3].wait_recv()
        accumulate(b, 2)
        gathers[b][4].wait_recv()
        gathers[b][5].wait_recv()
        accumulate(b, 3)

    ti = lax.broadcasted_iota(jnp.int32, (GROUP, GROUP), 0)
    si = lax.broadcasted_iota(jnp.int32, (GROUP, GROUP), 1)
    causal = ti >= si
    tri = jnp.where(causal, 1.0, 0.0).astype(F32)
    lane = lax.broadcasted_iota(jnp.int32, (GROUP, LANES), 1)
    r.rate[...] = jnp.zeros_like(r.rate)
    r.rate[:, :heads] = rate[...]

    def column(ref, b, h):
        return jnp.sum(jnp.where(lane == h, ref[b], 0.0), axis=1, keepdims=True)

    def spread(ref, b, j):
        return jnp.where(lane < HEADDIM, column(ref, b, per * j), column(ref, b, per * j + 1))

    def prepare(b):
        rs = rows_of(b)
        stp = r.step[...]
        decay = -stp * r.rate[...]
        cum = jnp.dot(tri, decay, preferred_element_type=F32, precision=lax.Precision.HIGHEST)
        r.cum[b] = cum
        r.cumt[b] = cum.T
        r.stept[b] = stp.T
        starts = resets[:, b * GROUP : (b + 1) * GROUP].astype(F32)
        whole = jnp.broadcast_to(starts, (GROUP, GROUP))
        seg_c = jnp.sum(tri * starts, axis=1, keepdims=True)
        start_c = jnp.sum(jnp.where(ti == si, whole, 0.0), axis=1, keepdims=True)
        seg_r = jnp.sum(jnp.where(ti <= si, jnp.broadcast_to(start_c, (GROUP, GROUP)), 0.0), axis=0, keepdims=True)
        last = cum[GROUP - 1 :, :]
        r.keep[b] = jnp.where(seg_c == seg_c[GROUP - 1 :, :], jnp.exp(last - cum), 0.0) * stp
        r.enter[b] = jnp.where(seg_c == 0.0, jnp.exp(cum), 0.0)
        dots = dot_nt(r.mapped[rs, NSTATE:], r.mapped[rs, :NSTATE])
        r.score[b] = jnp.where(causal & (seg_c == seg_r), dots, 0.0)

    def states(b):
        rs = rows_of(b)
        turned = r.mapped[rs, :NSTATE].astype(F32).T.astype(BF16)

        def turn(j, _):
            cols = cols_of(j)
            scaled = (spread(r.keep, b, j) * r.inner[rs, cols].astype(F32)).astype(BF16)
            new = dot(turned, scaled)
            through = spread(r.enter, b, j)[GROUP - 1 :, :]
            r.thr[b, :, cols] = through
            if b:
                new = new + through * r.state[b - 1, :, cols]
            r.state[b, :, cols] = new
            if b == blocks - 1:

                @pl.when(pos == 0)
                def _():
                    combine(j, False)

            return 0

        lax.fori_loop(0, pairs, turn, 0)

    def down(c):
        return remote("seq", upper, r.leaving.at[c], r.arrived.at[c], r.c_send.at[c], r.c_recv.at[c])

    def combine(c, seen):
        cols = cols_of(c)
        value = r.state[blocks - 1, :, cols]
        if seen:
            factor = r.thr[0, :, cols]
            for b in range(1, blocks):
                factor = factor * r.thr[b, :, cols]
            value = value + factor * r.arrived[c].astype(F32)
        r.leaving[c] = value.astype(BF16)
        down(c).start()

    def receive(c):
        down(c).wait_recv()

        @pl.when(pos < chain - 1)
        def _():
            combine(c, True)

    early = pairs // 2

    def within(b):
        rs = rows_of(b)

        def turn(j, _):
            cols = cols_of(j)
            x = r.inner[rs, cols]
            parts = []
            for k in range(per):
                h = per * j + k
                gap = column(r.cum, b, h) - r.cumt[b, pl.ds(h, 1), :]
                weight = jnp.exp(jnp.minimum(gap, 0.0)) * r.score[b] * r.stept[b, pl.ds(h, 1), :]
                parts.append(dot(weight.astype(BF16), x))
            d = jnp.where(lane < HEADDIM, skip[per * j], skip[per * j + 1])
            r.y[rs, cols] = jnp.where(lane < HEADDIM, parts[0], parts[1]) + d * x.astype(F32)
            if b == blocks - 1:

                @pl.when((pos == 1) & (j >= early))
                def _():
                    receive(j - early)

            return 0

        lax.fori_loop(0, pairs, turn, 0)

    @pl.when(pos == 0)
    def _():
        r.arrived[...] = jnp.zeros_like(r.arrived)

    accumulate(0, 0)
    relay(0)
    project(0)
    prepare(0)
    states(0)
    for b in range(1, blocks):
        relay(b)
        within(b - 1)
        accumulate(b, 0)
        project(b)
        prepare(b)
        states(b)
    within(blocks - 1)

    r.sums[...] = jnp.zeros_like(r.sums)

    def finish(j, _):
        @pl.when((pos > 1) | ((pos == 1) & (j >= pairs - early)))
        def _():
            receive(j)

        cols = cols_of(j)
        incoming = r.arrived[j].astype(F32)
        for b in range(blocks):
            rs = rows_of(b)
            state = incoming + r.state[b - 1, :, cols] if b else incoming
            carried = dot(r.mapped[rs, NSTATE:], state.astype(BF16))
            value = r.y[rs, cols] + spread(r.enter, b, j) * carried
            gated = value * silu(r.gating[rs, cols].astype(F32))
            r.g[rs, cols] = (gated * gain[pl.ds(j, 1), :]).astype(BF16)
            r.sums[rs, :] = r.sums[rs, :] + gated * gated
            incoming = r.thr[b, :, cols] * incoming
        return 0

    lax.fori_loop(0, pairs, finish, 0)

    for copy in out_loads:
        copy.wait()
    small = [
        remote("head", to, r.squares, r.others.at[k], r.q_send.at[k], r.q_recv.at[k])
        for k, to in enumerate((across, along, corner))
    ]
    scatters = [
        [
            remote("head", to, r.sent.at[6 * b + k], r.back.at[6 * b + k], r.o_send.at[6 * b + k], r.o_recv.at[6 * b + k])
            for k, to in enumerate((across, along, across, along, along, across))
        ]
        for b in range(blocks)
    ]

    def put(b, k, value):
        r.sent[6 * b + k] = value.astype(BF16)
        scatters[b][k].start()

    def share(k, rs):
        return dot(r.g[rs, :], r.vw[k])

    def direct(b):
        lo, hi = pl.ds(b * GROUP, half), pl.ds(b * GROUP + half, half)
        put(b, 0, share(0, lo))
        put(b, 1, share(0, hi))
        put(b, 2, share(1, lo))
        put(b, 3, share(2, hi))

    def joined(b):
        lo, hi = pl.ds(b * GROUP, half), pl.ds(b * GROUP + half, half)
        value = share(2, lo)
        scatters[b][0].wait_recv()
        put(b, 4, value + r.back[6 * b].astype(F32))
        value = share(1, hi)
        scatters[b][1].wait_recv()
        put(b, 5, value + r.back[6 * b + 1].astype(F32))

    for b in range(blocks):
        direct(b)
        if b == 0:
            r.squares[...] = dot_nt(jnp.ones((8, LANES), F32), r.sums[...], lax.Precision.HIGHEST)
            for copy in small:
                copy.start()
        if b:
            joined(b - 1)
    joined(blocks - 1)
    own = r.y
    for b in range(blocks):
        own[rows_of(b), :depth] = share(3, rows_of(b))
    for copy in small:
        copy.wait_recv()
    squared = r.squares[...] + r.others[0] + r.others[1] + r.others[2]
    scale = lax.rsqrt(squared / total + EPS)
    r.sums[...] = jnp.broadcast_to(scale[:1, :], (LANES, rows)).T
    for b in range(blocks):
        for base, picks in ((b * GROUP, (2, 4)), (b * GROUP + half, (3, 5))):
            span = pl.ds(base, half)
            for k in picks:
                scatters[b][k].wait_recv()
            for i in range(depth // LANES):
                cols = slice(i * LANES, (i + 1) * LANES)
                value = own[span, cols]
                for k in picks:
                    value = value + r.back[6 * b + k, :, cols].astype(F32)
                out[span, cols] = (value * r.sums[span, :]).astype(BF16)

    for group in gathers + scatters + [small]:
        for copy in group:
            copy.wait_send()

    @pl.when(pos < chain - 1)
    def _():
        for c in range(pairs):
            down(c).wait_send()


def layer(chain, split, tokens, resets, w_x, w_z, w_bc, w_dt, dt_bias, decay_rate, d_skip, norm_gain, w_out):
    rows, depth = tokens.shape
    width, heads, both = w_x.shape[1], w_dt.shape[1], w_bc.shape[1]
    padded = -(-heads // LANES) * LANES
    blocks, pairs = rows // GROUP, width // LANES
    half = GROUP // 2
    vm, dma = pltpu.VMEM, pltpu.SemaphoreType.DMA
    scratch = dict(
        got=vm((3, rows, depth), BF16),
        vx=vm((4, depth, width), BF16),
        vz=vm((4, depth, width), BF16),
        vb=vm((4, depth, both), BF16),
        vw=vm((4, width, depth), BF16),
        acc_x=vm((GROUP, width), F32),
        acc_z=vm((GROUP, width), F32),
        acc_m=vm((GROUP, both), F32),
        acc_s=vm((GROUP, heads), F32),
        inner=vm((rows, width), BF16),
        gating=vm((rows, width), BF16),
        mapped=vm((rows, both), BF16),
        step=vm((GROUP, padded), F32),
        rate=vm((1, padded), F32),
        cum=vm((blocks, GROUP, padded), F32),
        cumt=vm((blocks, padded, GROUP), F32),
        stept=vm((blocks, padded, GROUP), F32),
        keep=vm((blocks, GROUP, padded), F32),
        enter=vm((blocks, GROUP, padded), F32),
        score=vm((blocks, GROUP, GROUP), F32),
        state=vm((blocks, NSTATE, width), F32),
        thr=vm((blocks, 1, width), F32),
        arrived=vm((pairs, NSTATE, LANES), BF16),
        leaving=vm((pairs, NSTATE, LANES), BF16),
        y=vm((rows, width), F32),
        g=vm((rows, width), BF16),
        sums=vm((rows, LANES), F32),
        squares=vm((8, rows), F32),
        others=vm((3, 8, rows), F32),
        sent=vm((6 * blocks, half, depth), BF16),
        back=vm((6 * blocks, half, depth), BF16),
        load=dma((12,)),
        load_out=dma((4,)),
        g_send=dma((6 * blocks,)),
        g_recv=dma((6 * blocks,)),
        c_send=dma((pairs,)),
        c_recv=dma((pairs,)),
        o_send=dma((6 * blocks,)),
        o_recv=dma((6 * blocks,)),
        q_send=dma((3,)),
        q_recv=dma((3,)),
    )
    return pl.pallas_call(
        functools.partial(kernel, chain, float(width * split), tuple(scratch)),
        out_shape=jax.ShapeDtypeStruct((rows, depth), BF16),
        in_specs=[VMEM, VMEM, ANY, ANY, ANY, VMEM, VMEM, VMEM, SMEM, VMEM, ANY],
        out_specs=VMEM,
        scratch_shapes=list(scratch.values()),
        compiler_params=pltpu.CompilerParams(
            collective_id=0, has_side_effects=True, vmem_limit_bytes=60 * 1024 * 1024
        ),
    )(
        tokens, resets.reshape(1, rows), w_x, w_z, w_bc, w_dt.T, dt_bias.reshape(1, heads),
        decay_rate.reshape(1, heads), d_skip, norm_gain.reshape(pairs, LANES), w_out,
    )


def solution(mesh):
    in_specs = (
        P(("batch", "seq"), "head"),
        P(("batch", "seq")),
        P(None, "head"),
        P(None, "head"),
        P(),
        P(None, "head"),
        P("head"),
        P("head"),
        P("head"),
        P("head"),
        P("head", None),
    )
    return jax.shard_map(
        functools.partial(layer, mesh.shape["seq"], mesh.shape["head"]),
        mesh=mesh,
        in_specs=in_specs,
        out_specs=P(("batch", "seq"), "head"),
        check_vma=False,
    )
```

profile of v0, /device:TPU:24, one launch (start us, length us, event | category | flops | bytes accessed | tf_op | source)
XLA Modules:
  0.0 77.6 jit_solution(2082091666327897509)
XLA Ops:
  0.0 75.6 %shard_map.109 = bf16[512,640]{1,0:T(8,128)(2,1)} custom-call(bf16[512,640]{1,0:T(8,128)(2,1)} %tok.1, s32[1,512]{1,0:T(1,128)} %bitcast.7, bf16[2560,1280]{1,0:T(8,128)(2,1)} %w_x.1, bf16[2560,1280]{1,0:T(8,128)(2,1)} %w_z.1, bf16[2560,256]{1,0:T(8,128)(2,1)} %w_bc.1, bf16[20,2560]{1,0:T(8,128)(2,1)} %bitcast.5, f32[1,20]{1,0:T(1,128)} %bitcast.8, ...), custom_call_target="tpu_custom_call" | custom-call | tf_op jit(solution)/shard_map/pallas_call | solution.py:449
  75.6 2.0 %copy.13 = bf16[512,640]{1,0:T(8,128)(2,1)} copy(bf16[512,640]{1,0:T(8,128)(2,1)} %shard_map.109) | data formatting | bytes 1310720
where the time goes:
time: 77.7 us; the launch traced here: 77.6 us
  Pallas kernels  75.6 us (97%)
  local copies, waits for them, and re-layouts  1.98 us (3%)
    pallas_call x1, Pallas kernels, layer(): pl.pallas_call(functools.partial(kernel, chain, float(width * split), tup...  75.6 us
    unnamed x1, local copies, waits for them, and re-layouts  1.98 us

commit v1 on v0

v1 whole, which is shorter than its diff:
```python
import functools
import math

import jax
import jax.numpy as jnp
from jax import lax
from jax.experimental import pallas as pl
from jax.experimental.pallas import tpu as pltpu
from jax.sharding import PartitionSpec as P

HEADDIM = 64
NSTATE = 128
GROUP = 256
LANES = 128
CHUNK = 128
WIDE = 256
F32 = jnp.float32
BF16 = jnp.bfloat16
MESH = pl.DeviceIdType.MESH
ANY = pl.BlockSpec(memory_space=pl.ANY)
EPS = 1e-05
LOG2E = math.log2(math.e)


def peers():
    me = lax.axis_index("head")
    across = me + 1 - 2 * lax.rem(me, 2)
    along = lax.rem(me + 2, 4)
    corner = lax.rem(across + 2, 4)
    return me, across, along, corner


def remote(axis, to, src, dst, send, recv):
    return pltpu.make_async_remote_copy(
        src_ref=src, dst_ref=dst, send_sem=send, recv_sem=recv, device_id={axis: to}, device_id_type=MESH
    )


def silu(v):
    return v / (1.0 + jnp.exp(-v))


class Scratch:
    def __init__(self, names, refs):
        for name, ref in zip(names, refs):
            setattr(self, name, ref)


def dot(a, b):
    return jnp.dot(a, b, preferred_element_type=F32)


def dot_nt(a, b, precision=None):
    return lax.dot_general(a, b, (((1,), (1,)), ((), ())), preferred_element_type=F32, precision=precision)


def two_terms(v):
    high = v.astype(BF16)
    return jnp.concatenate([high, (v - high.astype(F32)).astype(BF16)], axis=1)


def kernel(chain, total, names, tok, resets, w_x, w_z, w_bc, w_dt, bias, rate, skip, gain, w_out, out, *refs):
    r = Scratch(names, refs)
    me, across, along, corner = peers()
    pos = lax.axis_index("seq")
    upper, lower = lax.rem(pos + 1, chain), lax.rem(pos + chain - 1, chain)
    rows, depth = tok.shape
    width = w_x.shape[1]
    heads = w_dt.shape[0]
    blocks, pairs, per = rows // GROUP, width // LANES, LANES // HEADDIM
    half = GROUP // 2
    chunks, parts = rows // CHUNK, GROUP // CHUNK
    first = 3 * depth // WIDE * WIDE
    owners = (me, across, along, corner)
    tiles = [slice(i, min(i + WIDE, width)) for i in range(0, width, WIDE)]

    def span_of(owner):
        return pl.ds(pl.multiple_of(owner * depth, LANES), depth)

    def place(k):
        return slice(k * depth, (k + 1) * depth)

    def rows_of(b):
        return slice(b * GROUP, (b + 1) * GROUP)

    def chunk_rows(i):
        return slice(i * CHUNK, (i + 1) * CHUNK)

    own_tokens = pltpu.make_async_copy(tok, r.xt.at[:, place(0)], r.small_load.at[0])
    own_tokens.start()
    barrier = pltpu.get_barrier_semaphore()
    for other in (across, along):
        pl.semaphore_signal(barrier, inc=1, device_id={"head": other}, device_id_type=MESH)
    for other in (upper, lower):
        pl.semaphore_signal(barrier, inc=1, device_id={"seq": other}, device_id_type=MESH)
    smalls = [
        pltpu.make_async_copy(src, dst, r.small_load.at[1 + i])
        for i, (src, dst) in enumerate(
            (
                (resets, r.resets), (w_dt, r.w_dt), (bias, r.bias0), (rate, r.rate0), (skip, r.skip0), (gain, r.gain),
            )
        )
    ]
    for copy in smalls:
        copy.start()
    loads = [
        (
            pltpu.make_async_copy(w_x.at[span_of(owner)], r.vx.at[place(k)], r.load.at[3 * k]),
            pltpu.make_async_copy(w_z.at[span_of(owner)], r.vz.at[place(k)], r.load.at[3 * k + 1]),
            pltpu.make_async_copy(w_bc.at[span_of(owner)], r.vb.at[place(k)], r.load.at[3 * k + 2]),
        )
        for k, owner in enumerate(owners)
    ]
    order = (corner, across, along, me)
    out_loads = [
        pltpu.make_async_copy(w_out.at[:, span_of(owner)], r.vw.at[k], r.load_out.at[k])
        for k, owner in enumerate(order)
    ]
    for group in loads:
        for copy in group:
            copy.start()

    gathers = []
    for b in range(blocks):
        lo = slice(b * GROUP, b * GROUP + half)
        hi = slice(b * GROUP + half, (b + 1) * GROUP)
        plan = (
            (across, r.xt.at[lo, place(0)], r.xt.at[lo, place(1)]),
            (along, r.xt.at[hi, place(0)], r.xt.at[hi, place(2)]),
            (across, r.xt.at[hi, place(0)], r.xt.at[hi, place(1)]),
            (along, r.xt.at[lo, place(0)], r.xt.at[lo, place(2)]),
            (along, r.xt.at[lo, place(1)], r.xt.at[lo, place(3)]),
            (across, r.xt.at[hi, place(2)], r.xt.at[hi, place(3)]),
        )
        gathers.append([
            remote("head", to, src, dst, r.g_send.at[6 * b + i], r.g_recv.at[6 * b + i])
            for i, (to, src, dst) in enumerate(plan)
        ])
    own_tokens.wait()
    pl.semaphore_wait(barrier, 4)
    for copy in gathers[0][:4]:
        copy.start()

    ti = lax.broadcasted_iota(jnp.int32, (CHUNK, CHUNK), 0)
    si = lax.broadcasted_iota(jnp.int32, (CHUNK, CHUNK), 1)
    causal = ti >= si
    tri = jnp.where(causal, 1.0, 0.0).astype(F32)
    left = si < HEADDIM
    for k in range(3):
        r.tri[:, k * CHUNK : (k + 1) * CHUNK] = tri.astype(BF16)
    for cols in tiles:
        shape = (2 * LANES, cols.stop - cols.start)
        channel = lax.broadcasted_iota(jnp.int32, shape, 1) + cols.start
        source = lax.rem(lax.broadcasted_iota(jnp.int32, shape, 0), LANES)
        inside = (channel >= source * HEADDIM) & (channel < (source + 1) * HEADDIM)
        r.widen[:, cols] = jnp.where(inside, 1.0, 0.0).astype(BF16)
    for copy in smalls:
        copy.wait()
    r.rate[...] = jnp.zeros_like(r.rate)
    r.rate[:, :heads] = r.rate0[...] * LOG2E
    r.bias[...] = jnp.zeros_like(r.bias)
    r.bias[:, :heads] = r.bias0[...]
    r.skip[...] = jnp.zeros_like(r.skip)
    r.skip[:, :heads] = r.skip0[...]
    r.wd[...] = jnp.zeros_like(r.wd)
    for k, owner in enumerate(owners):
        r.wd[:heads, place(k)] = r.w_dt[:, span_of(owner)]
    spare = jnp.broadcast_to(r.skip[...], (8, LANES))
    for cols in tiles:
        r.skips[:, cols] = dot(two_terms(spare), r.widen[:, cols])
    seen = jnp.zeros((1, LANES), F32)
    for i in range(chunks):
        rs = chunk_rows(i)
        starts = r.resets[:, rs].astype(F32)
        seg = jnp.broadcast_to(jnp.sum(tri * starts, axis=1, keepdims=True), (CHUNK, CHUNK))
        last = seg[CHUNK - 1 :, :]
        r.mask[i] = jnp.where(causal & (seg == seg.T), 1.0, 0.0)
        r.alone[rs, :] = jnp.where(seg == 0.0, 1.0, 0.0)
        r.same[rs, :] = jnp.where(seg == last, 1.0, 0.0)
        r.open[rs, :] = jnp.where(seg + seen == 0.0, 1.0, 0.0)
        seen = seen + last

    def early(b, which):
        rs = rows_of(b)
        x = r.xt.at[rs, :first]
        if "x" in which:
            for cols in tiles:
                r.acc_x[:, cols] = dot(x[...], r.vx[:first, cols])
            r.acc_m[...] = dot(x[...], r.vb[:first, :])
            r.acc_s[...] = dot_nt(x[...], r.wd[:, :first])
        if "z" in which:
            for cols in tiles:
                r.acc_z[:, cols] = dot(x[...], r.vz[:first, cols])

    def late_small(b):
        rs = rows_of(b)
        x = r.xt.at[rs, first:]
        r.mapped[rs, :] = silu(r.acc_m[...] + dot(x[...], r.vb[first:, :])).astype(BF16)
        v = r.acc_s[...] + dot_nt(x[...], r.wd[:, first:]) + r.bias[...]
        r.step[...] = jnp.maximum(v, 0.0) + jnp.log1p(jnp.exp(-jnp.abs(v)))

    def late_x(b):
        rs = rows_of(b)
        x = r.xt.at[rs, first:]
        for cols in tiles:
            r.inner[rs, cols] = silu(r.acc_x[:, cols] + dot(x[...], r.vx[first:, cols])).astype(BF16)

    def late_z(b):
        rs = rows_of(b)
        x = r.xt.at[rs, first:]
        for cols in tiles:
            z = (r.acc_z[:, cols] + dot(x[...], r.vz[first:, cols])).astype(BF16).astype(F32)
            r.gate[rs, cols] = silu(z)

    def prepare(b):
        for i in range(b * parts, (b + 1) * parts):
            rs = chunk_rows(i)
            stp = r.step[(i - b * parts) * CHUNK : (i - b * parts + 1) * CHUNK, :]
            decay = -stp * r.rate[...]
            high = decay.astype(BF16)
            rest = decay - high.astype(F32)
            middle = rest.astype(BF16)
            low = (rest - middle.astype(F32)).astype(BF16)
            cum = dot(r.tri[...], jnp.concatenate([high, middle, low], axis=0))
            last = cum[CHUNK - 1 :, :]
            before = r.before[i : i + 1, :]
            r.before[i + 1 : i + 2, :] = before + last
            r.cum[i] = cum
            r.cumt[i] = cum.T
            r.stept[i] = stp.T
            r.keep[rs, :] = two_terms(r.same[rs, :] * jnp.exp2(last - cum) * stp)
            r.enter[rs, :] = two_terms(r.alone[rs, :] * jnp.exp2(cum))
            r.outer[rs, :] = two_terms(r.open[rs, :] * jnp.exp2(before + cum))
            mapped_b, mapped_c = r.mapped[rs, :NSTATE], r.mapped[rs, NSTATE:]
            r.score[i] = r.mask[i] * dot_nt(mapped_c, mapped_b)
            r.turned[i] = mapped_b.astype(F32).T.astype(BF16)

    def down(c):
        return remote("seq", upper, r.leaving.at[c], r.arrived.at[c], r.c_send.at[c], r.c_recv.at[c])

    def states(i):
        rs = chunk_rows(i)
        for cols in tiles:
            scaled = (dot(r.keep[rs, :], r.widen[:, cols]) * r.inner[rs, cols].astype(F32)).astype(BF16)
            new = dot(r.turned[i], scaled)
            if i:
                through = dot(r.enter[rs.stop - 16 : rs.stop, :], r.widen[:, cols])[15:, :]
                new = new + through * r.state[i, :, cols]
            r.state[i + 1, :, cols] = new
            if i == chunks - 1:
                spans = [slice(c, c + LANES) for c in range(cols.start, cols.stop, LANES)]
                for span in spans:
                    r.leaving[span.start // LANES] = r.state[chunks, :, span].astype(BF16)

                @pl.when((pos == 0) & (pos < chain - 1))
                def _():
                    for span in spans:
                        down(span.start // LANES).start()

    def within(i):
        rs = chunk_rows(i)
        own_c = r.mapped[rs, NSTATE:]
        for cols in tiles:
            outer = dot(r.outer[rs, :], r.widen[:, cols])
            r.factor[rs, cols] = outer * r.gate[rs, cols]
            rest = r.skips[:1, cols] * r.inner[rs, cols].astype(F32)
            if i:
                carried = dot(own_c, r.state[i, :, cols].astype(BF16))
                rest = rest + dot(r.enter[rs, :], r.widen[:, cols]) * carried
            r.y[rs, cols] = rest
        for j in range(pairs):
            cols = slice(j * LANES, (j + 1) * LANES)
            x = r.inner[rs, cols]
            weights = []
            for h in range(per * j, per * (j + 1)):
                gap = r.cum[i, :, h : h + 1] - r.cumt[i, h : h + 1, :]
                weight = jnp.exp2(jnp.minimum(gap, 0.0)) * r.score[i] * r.stept[i, h : h + 1, :]
                weights.append(weight.astype(BF16))
            zero = jnp.zeros_like(x)
            split = jnp.concatenate([jnp.where(left, x, zero), jnp.where(left, zero, x)], axis=0)
            inside = dot(jnp.concatenate(weights, axis=1), split)
            r.y[rs, cols] = (r.y[rs, cols] + inside) * r.gate[rs, cols]

    r.before[...] = jnp.zeros_like(r.before)

    @pl.when(pos == 0)
    def _():
        r.arrived[...] = jnp.zeros_like(r.arrived)

    def relay(b):
        gathers[b][0].wait_recv()
        gathers[b][4].start()
        gathers[b][1].wait_recv()
        gathers[b][5].start()
        if b + 1 < blocks:
            for copy in gathers[b + 1][:4]:
                copy.start()

    def direct_here(b):
        gathers[b][2].wait_recv()
        gathers[b][3].wait_recv()

    def relayed_here(b):
        gathers[b][4].wait_recv()
        gathers[b][5].wait_recv()

    relay(0)
    for k in range(3):
        for copy in loads[k]:
            copy.wait()
    for b in range(blocks):
        final = b == blocks - 1
        direct_here(b)
        early(b, "x")
        early(b, "z")
        if b == 0:
            for copy in loads[3]:
                copy.wait()
            for copy in out_loads:
                copy.start()
        relayed_here(b)
        late_small(b)
        prepare(b)
        late_x(b)
        if not final:
            late_z(b)
        for i in range(b * parts, (b + 1) * parts):
            states(i)
        if final:
            late_z(b)
        for i in range(b * parts, (b + 1) * parts):
            within(i)
            if not final and i == b * parts:
                relay(b + 1)

    r.sums[...] = jnp.zeros_like(r.sums)

    def finish(c, _):
        cols = pl.ds(pl.multiple_of(c * LANES, LANES), LANES)

        @pl.when(pos > 0)
        def _():
            down(c).wait_recv()

            @pl.when(pos < chain - 1)
            def _():
                through = dot(r.outer[rows - 16 :, :], r.widen[:, cols])[15:, :]
                value = r.state[chunks, :, cols] + through * r.arrived[c].astype(F32)
                r.leaving[c] = value.astype(BF16)
                down(c).start()

        carried = dot(r.mapped[:, NSTATE:], r.arrived[c])
        gated = r.y[:, cols] + r.factor[:, cols] * carried
        r.g[:, cols] = (gated * r.gain[:, cols]).astype(BF16)
        r.sums[...] = r.sums[...] + gated * gated
        return 0

    lax.fori_loop(0, pairs, finish, 0)

    for copy in out_loads:
        copy.wait()
    small = [
        remote("head", to, r.squares.at[k], r.others.at[k], r.q_send.at[k], r.q_recv.at[k])
        for k, to in enumerate((across, along))
    ]
    scatters = [
        [
            remote("head", to, r.sent.at[6 * b + k], r.back.at[6 * b + k], r.o_send.at[6 * b + k], r.o_recv.at[6 * b + k])
            for k, to in enumerate((across, along, across, along, along, across))
        ]
        for b in range(blocks)
    ]

    def put(b, k, value):
        r.sent[6 * b + k] = value.astype(BF16)
        scatters[b][k].start()

    def share(k, rs):
        return dot(r.g[rs, :], r.vw[k])

    def direct(b):
        lo, hi = slice(b * GROUP, b * GROUP + half), slice(b * GROUP + half, (b + 1) * GROUP)
        put(b, 0, share(0, lo))
        put(b, 1, share(0, hi))
        put(b, 2, share(1, lo))
        put(b, 3, share(2, hi))

    def joined(b):
        lo, hi = slice(b * GROUP, b * GROUP + half), slice(b * GROUP + half, (b + 1) * GROUP)
        value = share(2, lo)
        scatters[b][0].wait_recv()
        put(b, 4, value + r.back[6 * b].astype(F32))
        value = share(1, hi)
        scatters[b][1].wait_recv()
        put(b, 5, value + r.back[6 * b + 1].astype(F32))

    slot = lax.broadcasted_iota(jnp.int32, (8, LANES), 0)
    for b in range(blocks):
        direct(b)
        if b == 0:
            squares = jnp.zeros((8, LANES), F32)
            for i in range(chunks):
                row = dot_nt(jnp.ones((8, LANES), F32), r.sums[chunk_rows(i), :], lax.Precision.HIGHEST)
                squares = jnp.where(slot == i, row, squares)
            r.squares[0] = squares
            small[0].start()
        if b:
            joined(b - 1)
    small[0].wait_recv()
    r.squares[1] = r.squares[0] + r.others[0]
    small[1].start()
    joined(blocks - 1)
    own = r.y
    for b in range(blocks):
        own[rows_of(b), :depth] = share(3, rows_of(b))
    small[1].wait_recv()
    scale = lax.rsqrt((r.squares[1] + r.others[1]) / total + EPS)
    for i in range(chunks):
        r.sums[chunk_rows(i), :] = jnp.broadcast_to(scale[i : i + 1, :], (LANES, CHUNK)).T
    stores = []
    for b in range(blocks):
        for base, picks in ((b * GROUP, (2, 4)), (b * GROUP + half, (3, 5))):
            span = slice(base, base + half)
            for k in picks:
                scatters[b][k].wait_recv()
            for i in range(depth // LANES):
                cols = slice(i * LANES, (i + 1) * LANES)
                value = own[span, cols]
                for k in picks:
                    value = value + r.back[6 * b + k, :, cols].astype(F32)
                r.result[span, cols] = (value * r.sums[span, :]).astype(BF16)
            stores.append(pltpu.make_async_copy(r.result.at[span], out.at[span], r.store.at[len(stores)]))
            stores[-1].start()

    for group in gathers + scatters + [small]:
        for copy in group:
            copy.wait_send()

    @pl.when(pos < chain - 1)
    def _():
        for c in range(pairs):
            down(c).wait_send()

    for copy in stores:
        copy.wait()


def layer(chain, split, tokens, resets, w_x, w_z, w_bc, w_dt, dt_bias, decay_rate, d_skip, norm_gain, w_out):
    rows, depth = tokens.shape
    width, heads, both = w_x.shape[1], w_dt.shape[1], w_bc.shape[1]
    blocks, pairs = rows // GROUP, width // LANES
    chunks = rows // CHUNK
    half = GROUP // 2
    vm, dma = pltpu.VMEM, pltpu.SemaphoreType.DMA
    scratch = dict(
        xt=vm((rows, 4 * depth), BF16),
        vx=vm((4 * depth, width), BF16),
        vz=vm((4 * depth, width), BF16),
        vb=vm((4 * depth, both), BF16),
        vw=vm((4, width, depth), BF16),
        wd=vm((LANES, 4 * depth), BF16),
        w_dt=vm((heads, 4 * depth), BF16),
        resets=vm((1, rows), jnp.int32),
        bias0=vm((1, heads), F32),
        rate0=vm((1, heads), F32),
        skip0=vm((1, heads), F32),
        bias=vm((1, LANES), F32),
        rate=vm((1, LANES), F32),
        skip=vm((1, LANES), F32),
        skips=vm((8, width), F32),
        gain=vm((1, width), F32),
        tri=vm((CHUNK, 3 * CHUNK), BF16),
        widen=vm((2 * LANES, width), BF16),
        mask=vm((chunks, CHUNK, CHUNK), F32),
        alone=vm((rows, LANES), F32),
        same=vm((rows, LANES), F32),
        open=vm((rows, LANES), F32),
        acc_x=vm((GROUP, width), F32),
        acc_z=vm((GROUP, width), F32),
        acc_m=vm((GROUP, both), F32),
        acc_s=vm((GROUP, LANES), F32),
        inner=vm((rows, width), BF16),
        gate=vm((rows, width), F32),
        mapped=vm((rows, both), BF16),
        turned=vm((chunks, NSTATE, CHUNK), BF16),
        step=vm((GROUP, LANES), F32),
        before=vm((chunks + 1, LANES), F32),
        cum=vm((chunks, CHUNK, LANES), F32),
        cumt=vm((chunks, LANES, CHUNK), F32),
        stept=vm((chunks, LANES, CHUNK), F32),
        keep=vm((rows, 2 * LANES), BF16),
        enter=vm((rows, 2 * LANES), BF16),
        outer=vm((rows, 2 * LANES), BF16),
        score=vm((chunks, CHUNK, CHUNK), F32),
        state=vm((chunks + 1, NSTATE, width), F32),
        arrived=vm((pairs, NSTATE, LANES), BF16),
        leaving=vm((pairs, NSTATE, LANES), BF16),
        y=vm((rows, width), F32),
        factor=vm((rows, width), F32),
        g=vm((rows, width), BF16),
        sums=vm((rows, LANES), F32),
        squares=vm((2, 8, LANES), F32),
        others=vm((2, 8, LANES), F32),
        sent=vm((6 * blocks, half, depth), BF16),
        back=vm((6 * blocks, half, depth), BF16),
        result=vm((rows, depth), BF16),
        small_load=dma((7,)),
        load=dma((12,)),
        load_out=dma((4,)),
        g_send=dma((6 * blocks,)),
        g_recv=dma((6 * blocks,)),
        c_send=dma((pairs,)),
        c_recv=dma((pairs,)),
        o_send=dma((6 * blocks,)),
        o_recv=dma((6 * blocks,)),
        q_send=dma((2,)),
        q_recv=dma((2,)),
        store=dma((2 * blocks,)),
    )
    return pl.pallas_call(
        functools.partial(kernel, chain, float(width * split), tuple(scratch)),
        out_shape=jax.ShapeDtypeStruct((rows, depth), BF16),
        in_specs=[ANY] * 11,
        out_specs=ANY,
        scratch_shapes=list(scratch.values()),
        compiler_params=pltpu.CompilerParams(
            collective_id=0, has_side_effects=True, vmem_limit_bytes=60 * 1024 * 1024
        ),
    )(
        tokens, resets.reshape(1, rows), w_x, w_z, w_bc, w_dt.T, dt_bias.reshape(1, heads),
        decay_rate.reshape(1, heads), d_skip.reshape(1, heads), norm_gain.reshape(1, width), w_out,
    )


def solution(mesh):
    in_specs = (
        P(("batch", "seq"), "head"),
        P(("batch", "seq")),
        P(None, "head"),
        P(None, "head"),
        P(),
        P(None, "head"),
        P("head"),
        P("head"),
        P("head"),
        P("head"),
        P("head", None),
    )
    return jax.shard_map(
        functools.partial(layer, mesh.shape["seq"], mesh.shape["head"]),
        mesh=mesh,
        in_specs=in_specs,
        out_specs=P(("batch", "seq"), "head"),
        check_vma=False,
    )
```

time: 77.7 us -> 67.3 us (0.87)
  Pallas kernels: 75.6 us -> 63.8 us
  local copies, waits for them, and re-layouts: 1.98 us -> 3.27 us
    pallas_call x1, Pallas kernels: 75.6 us -> 63.8 us  [layer(): pl.pallas_call(functools.partial(kernel, chain, float(width * split), tup...]
    reshape x0 -> x1, local copies, waits for them, and re-layouts: none -> 1.29 us  [layer(): norm_gain.reshape(1, width)]
where the time goes in v1:
time: 67.3 us; the launch traced here: 67.1 us
  Pallas kernels  63.8 us (95%)
  local copies, waits for them, and re-layouts  3.27 us (5%)
    pallas_call x1, Pallas kernels, layer(): pl.pallas_call(functools.partial(kernel, chain, float(width * split), tup...  63.8 us
    unnamed x1, local copies, waits for them, and re-layouts  1.98 us

profile of v1, /device:TPU:24, one launch (start us, length us, event | category | flops | bytes accessed | tf_op | source)
XLA Modules:
  0.0 67.1 jit_solution(13898318728177474298)
XLA Ops:
  0.0 1.3 %reshape.19.gain = f32[1,1280]{1,0:T(1,128)} reshape(f32[1280]{0:T(1024)} %param.20) | data formatting | bytes 10240 | tf_op jit(solution)/shard_map/reshape | solution.py:531
  1.3 63.8 %shard_map.109 = bf16[512,640]{1,0:T(8,128)(2,1)} custom-call(bf16[512,640]{1,0:T(8,128)(2,1)} %tok.1, s32[1,512]{1,0:T(1,128)} %bitcast.6, bf16[2560,1280]{1,0:T(8,128)(2,1)} %w_x.1, bf16[2560,1280]{1,0:T(8,128)(2,1)} %w_z.1, bf16[2560,256]{1,0:T(8,128)(2,1)} %w_bc.1, bf16[20,2560]{1,0:T(8,128)(2,1)} %bitcast.5, f32[1,20]{1,0:T(1,128)} %bitcast.7, ...), custom_call_target="tpu_custom_call" | custom-call | tf_op jit(solution)/shard_map/pallas_call | solution.py:520
  65.1 2.0 %copy.13 = bf16[512,640]{1,0:T(8,128)(2,1)} copy(bf16[512,640]{1,0:T(8,128)(2,1)} %shard_map.109) | data formatting | bytes 1310720

commit v2 on v1

--- a/solution.py
+++ b/solution.py
@@ -59,7 +59,7 @@
     return jnp.concatenate([high, (v - high.astype(F32)).astype(BF16)], axis=1)
 
 
-def kernel(chain, total, names, tok, resets, w_x, w_z, w_bc, w_dt, bias, rate, skip, gain, w_out, out, *refs):
+def kernel(chain, cores, total, names, tok, resets, w_x, w_z, w_bc, w_dt, bias, rate, skip, gain, w_out, out, *refs):
     r = Scratch(names, refs)
     me, across, along, corner = peers()
     pos = lax.axis_index("seq")
@@ -67,10 +67,11 @@
     rows, depth = tok.shape
     width = w_x.shape[1]
     heads = w_dt.shape[0]
+    core, other_core = lax.axis_index("batch"), 1 - lax.axis_index("batch")
     blocks, pairs, per = rows // GROUP, width // LANES, LANES // HEADDIM
     half = GROUP // 2
     chunks, parts = rows // CHUNK, GROUP // CHUNK
-    first = 3 * depth // WIDE * WIDE
+    cuts = (0, depth // WIDE * WIDE, 3 * depth // WIDE * WIDE, 4 * depth)
     owners = (me, across, along, corner)
     tiles = [slice(i, min(i + WIDE, width)) for i in range(0, width, WIDE)]
 
@@ -93,11 +94,13 @@
         pl.semaphore_signal(barrier, inc=1, device_id={"head": other}, device_id_type=MESH)
     for other in (upper, lower):
         pl.semaphore_signal(barrier, inc=1, device_id={"seq": other}, device_id_type=MESH)
+    if cores == 2:
+        pl.semaphore_signal(barrier, inc=1, device_id={"batch": other_core}, device_id_type=MESH)
     smalls = [
         pltpu.make_async_copy(src, dst, r.small_load.at[1 + i])
         for i, (src, dst) in enumerate(
             (
-                (resets, r.resets), (w_dt, r.w_dt), (bias, r.bias0), (rate, r.rate0), (skip, r.skip0), (gain, r.gain),
+                (resets, r.resets), (w_dt, r.w_dt), (bias, r.bias0), (rate, r.rate0), (skip, r.skip0), (gain, r.gain0),
             )
         )
     ]
@@ -137,9 +140,18 @@
             for i, (to, src, dst) in enumerate(plan)
         ])
     own_tokens.wait()
-    pl.semaphore_wait(barrier, 4)
-    for copy in gathers[0][:4]:
-        copy.start()
+    pl.semaphore_wait(barrier, 4 + cores // 2)
+
+    def send_first():
+        for copy in gathers[0][:4]:
+            copy.start()
+        for copies in gathers[1:]:
+            for copy in copies[:2]:
+                copy.start()
+
+    @pl.when(core == 0)
+    def _():
+        send_first()
 
     ti = lax.broadcasted_iota(jnp.int32, (CHUNK, CHUNK), 0)
     si = lax.broadcasted_iota(jnp.int32, (CHUNK, CHUNK), 1)
@@ -165,6 +177,8 @@
     r.wd[...] = jnp.zeros_like(r.wd)
     for k, owner in enumerate(owners):
         r.wd[:heads, place(k)] = r.w_dt[:, span_of(owner)]
+    for j in range(pairs):
+        r.gain[:, j * LANES : (j + 1) * LANES] = r.gain0[j : j + 1, :]
     spare = jnp.broadcast_to(r.skip[...], (8, LANES))
     for cols in tiles:
         r.skips[:, cols] = dot(two_terms(spare), r.widen[:, cols])
@@ -180,39 +194,40 @@
         r.open[rs, :] = jnp.where(seg + seen == 0.0, 1.0, 0.0)
         seen = seen + last
 
-    def early(b, which):
-        rs = rows_of(b)
-        x = r.xt.at[rs, :first]
-        if "x" in which:
+    def projected(b, k, what):
+        rs, span = rows_of(b), slice(cuts[k], cuts[k + 1])
+
+        def add(acc, cols, value):
+            acc[rs, cols] = value if k == 0 else acc[rs, cols] + value
+
+        if "x" in what:
+            add(r.acc_m, slice(None), dot(r.xt[rs, span], r.vb[span, :]))
+            add(r.acc_s, slice(None), dot_nt(r.xt[rs, span], r.wd[:, span]))
             for cols in tiles:
-                r.acc_x[:, cols] = dot(x[...], r.vx[:first, cols])
-            r.acc_m[...] = dot(x[...], r.vb[:first, :])
-            r.acc_s[...] = dot_nt(x[...], r.wd[:, :first])
-        if "z" in which:
+                add(r.acc_x, cols, dot(r.xt[rs, span], r.vx[span, cols]))
+        if "z" in what:
             for cols in tiles:
-                r.acc_z[:, cols] = dot(x[...], r.vz[:first, cols])
+                add(r.acc_z, cols, dot(r.xt[rs, span], r.vz[span, cols]))
 
     def late_small(b):
-        rs = rows_of(b)
-        x = r.xt.at[rs, first:]
-        r.mapped[rs, :] = silu(r.acc_m[...] + dot(x[...], r.vb[first:, :])).astype(BF16)
-        v = r.acc_s[...] + dot_nt(x[...], r.wd[:, first:]) + r.bias[...]
+        rs, span = rows_of(b), slice(cuts[2], cuts[3])
+        x = r.xt.at[rs, span]
+        r.mapped[rs, :] = silu(r.acc_m[rs, :] + dot(x[...], r.vb[span, :])).astype(BF16)
+        v = r.acc_s[rs, :] + dot_nt(x[...], r.wd[:, span]) + r.bias[...]
         r.step[...] = jnp.maximum(v, 0.0) + jnp.log1p(jnp.exp(-jnp.abs(v)))
 
-    def late_x(b):
-        rs = rows_of(b)
-        x = r.xt.at[rs, first:]
+    def late_x(b, cols):
+        rs, span = rows_of(b), slice(cuts[2], cuts[3])
+        r.inner[rs, cols] = silu(r.acc_x[rs, cols] + dot(r.xt[rs, span], r.vx[span, cols])).astype(BF16)
+
+    def late_z(b):
+        rs, span = rows_of(b), slice(cuts[2], cuts[3])
         for cols in tiles:
-            r.inner[rs, cols] = silu(r.acc_x[:, cols] + dot(x[...], r.vx[first:, cols])).astype(BF16)
-
-    def late_z(b):
-        rs = rows_of(b)
-        x = r.xt.at[rs, first:]
-        for cols in tiles:
-            z = (r.acc_z[:, cols] + dot(x[...], r.vz[first:, cols])).astype(BF16).astype(F32)
+            z = (r.acc_z[rs, cols] + dot(r.xt[rs, span], r.vz[span, cols])).astype(BF16).astype(F32)
             r.gate[rs, cols] = silu(z)
 
     def prepare(b):
+        leaves, through = [], None
         for i in range(b * parts, (b + 1) * parts):
             rs = chunk_rows(i)
             stp = r.step[(i - b * parts) * CHUNK : (i - b * parts + 1) * CHUNK, :]
@@ -228,34 +243,77 @@
             r.cum[i] = cum
             r.cumt[i] = cum.T
             r.stept[i] = stp.T
-            r.keep[rs, :] = two_terms(r.same[rs, :] * jnp.exp2(last - cum) * stp)
-            r.enter[rs, :] = two_terms(r.alone[rs, :] * jnp.exp2(cum))
-            r.outer[rs, :] = two_terms(r.open[rs, :] * jnp.exp2(before + cum))
+            keep = r.same[rs, :] * jnp.exp2(last - cum) * stp
+            r.keep[rs, :] = two_terms(keep)
+            enter = r.alone[rs, :] * jnp.exp2(cum)
+            outer = r.open[rs, :] * jnp.exp2(before + cum)
+            r.enter[rs, :] = two_terms(enter)
+            r.outer[rs, :] = two_terms(outer)
+            passed = enter[CHUNK - 1 :, :]
+            leaves = [value * passed for value in leaves] + [keep]
+            through = passed if through is None else through * passed
             mapped_b, mapped_c = r.mapped[rs, :NSTATE], r.mapped[rs, NSTATE:]
             r.score[i] = r.mask[i] * dot_nt(mapped_c, mapped_b)
-            r.turned[i] = mapped_b.astype(F32).T.astype(BF16)
+            turned = mapped_b.astype(F32).T.astype(BF16)
+            r.turned[b, :, (i - b * parts) * CHUNK : (i - b * parts + 1) * CHUNK] = turned
+        r.leave[...] = two_terms(jnp.concatenate(leaves, axis=0))
+        slot = lax.broadcasted_iota(jnp.int32, (8, LANES), 0)
+        ends = jnp.where(slot == 0, through, outer[CHUNK - 1 :, :])
+        r.ends[...] = two_terms(ends)
 
     def down(c):
         return remote("seq", upper, r.leaving.at[c], r.arrived.at[c], r.c_send.at[c], r.c_recv.at[c])
 
-    def states(i):
-        rs = chunk_rows(i)
+    def widened(ref, rs, cols):
+        return dot(ref[rs, :], r.widen[:, cols])
+
+    def block_state(b, cols):
+        rs = rows_of(b)
+        scaled = (dot(r.leave[...], r.widen[:, cols]) * r.inner[rs, cols].astype(F32)).astype(BF16)
+        new = dot(r.turned[b], scaled)
+        if b:
+            ends = dot(r.ends[...], r.widen[:, cols])
+            r.through[:, cols] = ends
+            new = new + ends[:1, :] * r.state[b - 1, :, cols]
+        r.state[b, :, cols] = new
+
+    def departures(cols):
+        return range(cols.start // LANES, cols.stop // LANES)
+
+    def leave_first(cols):
+        for c in departures(cols):
+            r.leaving[c] = r.state[blocks - 1, :, c * LANES : (c + 1) * LANES].astype(BF16)
+
+        @pl.when((pos == 0) & (pos < chain - 1))
+        def _():
+            for c in departures(cols):
+                down(c).start()
+
+    def pass_on(c, cols):
+        value = r.state[blocks - 1, :, cols] + r.through[1:2, cols] * r.arrived[c].astype(F32)
+        r.leaving[c] = value.astype(BF16)
+        down(c).start()
+
+    def slot(at, picks):
+        if picks and chain > at + 1:
+
+            @pl.when(pos == at)
+            def _():
+                for c in picks:
+                    down(c).wait_recv()
+                    pass_on(c, slice(c * LANES, (c + 1) * LANES))
+
+    def middle(i):
+        b = i // parts
+        rs = chunk_rows(i - 1)
+        turned = r.turned[b, :, (i - 1 - b * parts) * CHUNK : (i - b * parts) * CHUNK]
         for cols in tiles:
-            scaled = (dot(r.keep[rs, :], r.widen[:, cols]) * r.inner[rs, cols].astype(F32)).astype(BF16)
-            new = dot(r.turned[i], scaled)
-            if i:
-                through = dot(r.enter[rs.stop - 16 : rs.stop, :], r.widen[:, cols])[15:, :]
-                new = new + through * r.state[i, :, cols]
-            r.state[i + 1, :, cols] = new
-            if i == chunks - 1:
-                spans = [slice(c, c + LANES) for c in range(cols.start, cols.stop, LANES)]
-                for span in spans:
-                    r.leaving[span.start // LANES] = r.state[chunks, :, span].astype(BF16)
-
-                @pl.when((pos == 0) & (pos < chain - 1))
-                def _():
-                    for span in spans:
-                        down(span.start // LANES).start()
+            scaled = (widened(r.keep, rs, cols) * r.inner[rs, cols].astype(F32)).astype(BF16)
+            new = dot(turned, scaled)
+            if i > 1:
+                passed = dot(r.enter[rs.stop - 16 : rs.stop, :], r.widen[:, cols])[15:, :]
+                new = new + passed * (r.mid[...][:, cols] if (i - 1) % parts else r.state[b - 1, :, cols])
+            r.mid[:, cols] = new
 
     def within(i):
         rs = chunk_rows(i)
@@ -265,7 +323,8 @@
             r.factor[rs, cols] = outer * r.gate[rs, cols]
             rest = r.skips[:1, cols] * r.inner[rs, cols].astype(F32)
             if i:
-                carried = dot(own_c, r.state[i, :, cols].astype(BF16))
+                start = r.mid[:, cols] if i % parts else r.state[i // parts - 1, :, cols]
+                carried = dot(own_c, start.astype(BF16))
                 rest = rest + dot(r.enter[rs, :], r.widen[:, cols]) * carried
             r.y[rs, cols] = rest
         for j in range(pairs):
@@ -293,7 +352,7 @@
         gathers[b][1].wait_recv()
         gathers[b][5].start()
         if b + 1 < blocks:
-            for copy in gathers[b + 1][:4]:
+            for copy in gathers[b + 1][2:4]:
                 copy.start()
 
     def direct_here(b):
@@ -304,50 +363,87 @@
         gathers[b][4].wait_recv()
         gathers[b][5].wait_recv()
 
+    for copy in loads[0]:
+        copy.wait()
+    for b in range(blocks):
+        projected(b, 0, "xz")
+    if cores == 2:
+
+        @pl.when(core == 1)
+        def _():
+            pl.semaphore_wait(r.go.at[0], 1)
+            send_first()
+
     relay(0)
-    for k in range(3):
+    for k in (1, 2):
         for copy in loads[k]:
             copy.wait()
     for b in range(blocks):
-        final = b == blocks - 1
         direct_here(b)
-        early(b, "x")
-        early(b, "z")
+        projected(b, 1, "x")
         if b == 0:
+            projected(b, 1, "z")
             for copy in loads[3]:
                 copy.wait()
             for copy in out_loads:
                 copy.start()
+        if b + 1 < blocks:
+            relay(b + 1)
         relayed_here(b)
         late_small(b)
         prepare(b)
-        late_x(b)
-        if not final:
-            late_z(b)
-        for i in range(b * parts, (b + 1) * parts):
-            states(i)
-        if final:
-            late_z(b)
-        for i in range(b * parts, (b + 1) * parts):
-            within(i)
-            if not final and i == b * parts:
-                relay(b + 1)
+        if b == 0 and cores == 2:
+
+            @pl.when(core == 0)
+            def _():
+                pl.semaphore_signal(r.go.at[0], inc=1, device_id={"batch": other_core}, device_id_type=MESH)
+
+        if b + 1 < blocks:
+            for cols in tiles:
+                late_x(b, cols)
+            for cols in tiles:
+                block_state(b, cols)
+        else:
+            late_x(b, tiles[0])
+            for k, cols in enumerate(tiles):
+                if k + 1 < len(tiles):
+                    late_x(b, tiles[k + 1])
+                block_state(b, cols)
+                leave_first(cols)
+
+    picks = [range(pairs * k // 10, pairs * (k + 1) // 10) for k in range(10)]
+
+    def picked(low, high):
+        return [c for k in range(low, high) for c in picks[k]]
+
+    late_count = pairs * 8 // 10
+    late_z(0)
+    for b in range(1, blocks):
+        projected(b, 1, "z")
+    slot(1, picked(0, 1))
+    for b in range(1, blocks):
+        late_z(b)
+    slot(1, picked(1, 4))
+    passes = {0: ((4, 6), (0, 0)), 1: ((6, 10), (0, 2)), 2: ((0, 0), (2, 5)), 3: ((0, 0), (5, 8))}
+    for i in range(chunks):
+        if i % parts:
+            middle(i)
+        within(i)
+        for at in (1, 2):
+            slot(at, picked(*passes[i][at - 1]))
 
     r.sums[...] = jnp.zeros_like(r.sums)
 
     def finish(c, _):
         cols = pl.ds(pl.multiple_of(c * LANES, LANES), LANES)
 
-        @pl.when(pos > 0)
+        @pl.when((pos > 2) | ((pos == 2) & (c >= late_count)) | ((pos > 0) & (pos == chain - 1)))
         def _():
             down(c).wait_recv()
 
             @pl.when(pos < chain - 1)
             def _():
-                through = dot(r.outer[rows - 16 :, :], r.widen[:, cols])[15:, :]
-                value = r.state[chunks, :, cols] + through * r.arrived[c].astype(F32)
-                r.leaving[c] = value.astype(BF16)
-                down(c).start()
+                pass_on(c, cols)
 
         carried = dot(r.mapped[:, NSTATE:], r.arrived[c])
         gated = r.y[:, cols] + r.factor[:, cols] * carried
@@ -417,7 +513,6 @@
     scale = lax.rsqrt((r.squares[1] + r.others[1]) / total + EPS)
     for i in range(chunks):
         r.sums[chunk_rows(i), :] = jnp.broadcast_to(scale[i : i + 1, :], (LANES, CHUNK)).T
-    stores = []
     for b in range(blocks):
         for base, picks in ((b * GROUP, (2, 4)), (b * GROUP + half, (3, 5))):
             span = slice(base, base + half)
@@ -428,9 +523,7 @@
                 value = own[span, cols]
                 for k in picks:
                     value = value + r.back[6 * b + k, :, cols].astype(F32)
-                r.result[span, cols] = (value * r.sums[span, :]).astype(BF16)
-            stores.append(pltpu.make_async_copy(r.result.at[span], out.at[span], r.store.at[len(stores)]))
-            stores[-1].start()
+                out[span, cols] = (value * r.sums[span, :]).astype(BF16)
 
     for group in gathers + scatters + [small]:
         for copy in group:
@@ -441,11 +534,8 @@
         for c in range(pairs):
             down(c).wait_send()
 
-    for copy in stores:
-        copy.wait()
-
-
-def layer(chain, split, tokens, resets, w_x, w_z, w_bc, w_dt, dt_bias, decay_rate, d_skip, norm_gain, w_out):
+
+def layer(chain, split, cores, tokens, resets, w_x, w_z, w_bc, w_dt, dt_bias, decay_rate, d_skip, norm_gain, w_out):
     rows, depth = tokens.shape
     width, heads, both = w_x.shape[1], w_dt.shape[1], w_bc.shape[1]
     blocks, pairs = rows // GROUP, width // LANES
@@ -468,6 +558,7 @@
         rate=vm((1, LANES), F32),
         skip=vm((1, LANES), F32),
         skips=vm((8, width), F32),
+        gain0=vm((pairs, LANES), F32),
         gain=vm((1, width), F32),
         tri=vm((CHUNK, 3 * CHUNK), BF16),
         widen=vm((2 * LANES, width), BF16),
@@ -475,14 +566,18 @@
         alone=vm((rows, LANES), F32),
         same=vm((rows, LANES), F32),
         open=vm((rows, LANES), F32),
-        acc_x=vm((GROUP, width), F32),
-        acc_z=vm((GROUP, width), F32),
-        acc_m=vm((GROUP, both), F32),
-        acc_s=vm((GROUP, LANES), F32),
+        acc_x=vm((rows, width), F32),
+        acc_z=vm((rows, width), F32),
+        acc_m=vm((rows, both), F32),
+        acc_s=vm((rows, LANES), F32),
         inner=vm((rows, width), BF16),
         gate=vm((rows, width), F32),
         mapped=vm((rows, both), BF16),
-        turned=vm((chunks, NSTATE, CHUNK), BF16),
+        turned=vm((blocks, NSTATE, GROUP), BF16),
+        leave=vm((GROUP, 2 * LANES), BF16),
+        ends=vm((8, 2 * LANES), BF16),
+        through=vm((8, width), F32),
+        mid=vm((NSTATE, width), F32),
         step=vm((GROUP, LANES), F32),
         before=vm((chunks + 1, LANES), F32),
         cum=vm((chunks, CHUNK, LANES), F32),
@@ -492,7 +587,7 @@
         enter=vm((rows, 2 * LANES), BF16),
         outer=vm((rows, 2 * LANES), BF16),
         score=vm((chunks, CHUNK, CHUNK), F32),
-        state=vm((chunks + 1, NSTATE, width), F32),
+        state=vm((blocks, NSTATE, width), F32),
         arrived=vm((pairs, NSTATE, LANES), BF16),
         leaving=vm((pairs, NSTATE, LANES), BF16),
         y=vm((rows, width), F32),
@@ -503,7 +598,6 @@
         others=vm((2, 8, LANES), F32),
         sent=vm((6 * blocks, half, depth), BF16),
         back=vm((6 * blocks, half, depth), BF16),
-        result=vm((rows, depth), BF16),
         small_load=dma((7,)),
         load=dma((12,)),
         load_out=dma((4,)),
@@ -515,20 +609,20 @@
         o_recv=dma((6 * blocks,)),
         q_send=dma((2,)),
         q_recv=dma((2,)),
-        store=dma((2 * blocks,)),
+        go=pltpu.SemaphoreType.REGULAR((1,)),
     )
     return pl.pallas_call(
-        functools.partial(kernel, chain, float(width * split), tuple(scratch)),
-        out_shape=jax.ShapeDtypeStruct((rows, depth), BF16),
+        functools.partial(kernel, chain, cores, float(width * split), tuple(scratch)),
+        out_shape=pltpu.VMEM((rows, depth), BF16),
         in_specs=[ANY] * 11,
-        out_specs=ANY,
+        out_specs=pl.BlockSpec(memory_space=pltpu.VMEM),
         scratch_shapes=list(scratch.values()),
         compiler_params=pltpu.CompilerParams(
             collective_id=0, has_side_effects=True, vmem_limit_bytes=60 * 1024 * 1024
         ),
     )(
         tokens, resets.reshape(1, rows), w_x, w_z, w_bc, w_dt.T, dt_bias.reshape(1, heads),
-        decay_rate.reshape(1, heads), d_skip.reshape(1, heads), norm_gain.reshape(1, width), w_out,
+        decay_rate.reshape(1, heads), d_skip.reshape(1, heads), norm_gain.reshape(pairs, LANES), w_out,
     )
 
 
@@ -547,7 +641,7 @@
         P("head", None),
     )
     return jax.shard_map(
-        functools.partial(layer, mesh.shape["seq"], mesh.shape["head"]),
+        functools.partial(layer, mesh.shape["seq"], mesh.shape["head"], mesh.shape["batch"]),
         mesh=mesh,
         in_specs=in_specs,
         out_specs=P(("batch", "seq"), "head"),

time: 67.3 us -> 59.1 us (0.88)
  the two profiles are of different devices: /device:TPU:24 before, /device:TPU:25 now
where the time goes in v2:
time: 59.1 us; the launch traced here: 59 us
  Pallas kernels  58.1 us (98%)
  local copies, waits for them, and re-layouts  0.84 us (1%)
    pallas_call x1, Pallas kernels, layer(): pl.pallas_call(functools.partial(kernel, chain, cores, float(width * spli...  58.1 us

profile of v2, /device:TPU:25, one launch (start us, length us, event | category | flops | bytes accessed | tf_op | source)
XLA Modules:
  0.0 59.0 jit_solution(15747034350514706183)
XLA Ops:
  0.0 58.1 %shard_map.109 = bf16[512,640]{1,0:T(8,128)(2,1)S(1)} custom-call(bf16[512,640]{1,0:T(8,128)(2,1)} %tok.1, s32[1,512]{1,0:T(1,128)} %bitcast.8, bf16[2560,1280]{1,0:T(8,128)(2,1)} %w_x.1, bf16[2560,1280]{1,0:T(8,128)(2,1)} %w_z.1, bf16[2560,256]{1,0:T(8,128)(2,1)} %w_bc.1, bf16[20,2560]{1,0:T(8,128)(2,1)} %bitcast.6, f32[1,20]{1,0:T(1,128)} %bitcast.9, ...), custom_call_target="tpu_custom_call" | custom-call | tf_op jit(solution)/shard_map/pallas_call | solution.py:614
  58.1 0.8 %copy.13 = bf16[512,640]{1,0:T(8,128)(2,1)} copy(bf16[512,640]{1,0:T(8,128)(2,1)S(1)} %shard_map.109) | data formatting | bytes 1310720

commit v3 on v2

--- a/solution.py
+++ b/solution.py
@@ -92,8 +92,11 @@
     barrier = pltpu.get_barrier_semaphore()
     for other in (across, along):
         pl.semaphore_signal(barrier, inc=1, device_id={"head": other}, device_id_type=MESH)
-    for other in (upper, lower):
-        pl.semaphore_signal(barrier, inc=1, device_id={"seq": other}, device_id_type=MESH)
+
+    @pl.when(pos > 0)
+    def _():
+        pl.semaphore_signal(barrier, inc=1, device_id={"seq": lower}, device_id_type=MESH)
+
     if cores == 2:
         pl.semaphore_signal(barrier, inc=1, device_id={"batch": other_core}, device_id_type=MESH)
     smalls = [
@@ -108,18 +111,18 @@
         copy.start()
     loads = [
         (
-            pltpu.make_async_copy(w_x.at[span_of(owner)], r.vx.at[place(k)], r.load.at[3 * k]),
-            pltpu.make_async_copy(w_z.at[span_of(owner)], r.vz.at[place(k)], r.load.at[3 * k + 1]),
-            pltpu.make_async_copy(w_bc.at[span_of(owner)], r.vb.at[place(k)], r.load.at[3 * k + 2]),
+            pltpu.make_async_copy(w_x.at[span_of(owner)], r.vx.at[place(k)], r.load.at[3 * (k % 3)]),
+            pltpu.make_async_copy(w_z.at[span_of(owner)], r.vz.at[place(k)], r.load.at[3 * (k % 3) + 1]),
+            pltpu.make_async_copy(w_bc.at[span_of(owner)], r.vb.at[place(k)], r.load.at[3 * (k % 3) + 2]),
         )
         for k, owner in enumerate(owners)
     ]
     order = (corner, across, along, me)
     out_loads = [
-        pltpu.make_async_copy(w_out.at[:, span_of(owner)], r.vw.at[k], r.load_out.at[k])
+        pltpu.make_async_copy(w_out.at[:, span_of(owner)], r.vw.at[k], r.load.at[3 + k])
         for k, owner in enumerate(order)
     ]
-    for group in loads:
+    for group in loads[:3]:
         for copy in group:
             copy.start()
 
@@ -136,11 +139,19 @@
             (across, r.xt.at[hi, place(2)], r.xt.at[hi, place(3)]),
         )
         gathers.append([
-            remote("head", to, src, dst, r.g_send.at[6 * b + i], r.g_recv.at[6 * b + i])
+            remote("head", to, src, dst, r.g_send.at[0], r.g_recv.at[4 * b + min(i, 2) + i // 4])
             for i, (to, src, dst) in enumerate(plan)
         ])
     own_tokens.wait()
-    pl.semaphore_wait(barrier, 4 + cores // 2)
+
+    @pl.when(pos < chain - 1)
+    def _():
+        pl.semaphore_wait(barrier, 3 + cores // 2)
+
+    @pl.when(pos == chain - 1)
+    def _():
+        pl.semaphore_wait(barrier, 2 + cores // 2)
+
 
     def send_first():
         for copy in gathers[0][:4]:
@@ -194,7 +205,9 @@
         r.open[rs, :] = jnp.where(seg + seen == 0.0, 1.0, 0.0)
         seen = seen + last
 
-    def projected(b, k, what):
+    some = len(tiles) // 2
+
+    def projected(b, k, what, part=None):
         rs, span = rows_of(b), slice(cuts[k], cuts[k + 1])
 
         def add(acc, cols, value):
@@ -206,7 +219,7 @@
             for cols in tiles:
                 add(r.acc_x, cols, dot(r.xt[rs, span], r.vx[span, cols]))
         if "z" in what:
-            for cols in tiles:
+            for cols in part or tiles:
                 add(r.acc_z, cols, dot(r.xt[rs, span], r.vz[span, cols]))
 
     def late_small(b):
@@ -220,9 +233,9 @@
         rs, span = rows_of(b), slice(cuts[2], cuts[3])
         r.inner[rs, cols] = silu(r.acc_x[rs, cols] + dot(r.xt[rs, span], r.vx[span, cols])).astype(BF16)
 
-    def late_z(b):
+    def late_z(b, part=None):
         rs, span = rows_of(b), slice(cuts[2], cuts[3])
-        for cols in tiles:
+        for cols in part or tiles:
             z = (r.acc_z[rs, cols] + dot(r.xt[rs, span], r.vz[span, cols])).astype(BF16).astype(F32)
             r.gate[rs, cols] = silu(z)
 
@@ -262,7 +275,7 @@
         r.ends[...] = two_terms(ends)
 
     def down(c):
-        return remote("seq", upper, r.leaving.at[c], r.arrived.at[c], r.c_send.at[c], r.c_recv.at[c])
+        return remote("seq", upper, r.leaving.at[c], r.arrived.at[c], r.c_send.at[0], r.c_recv.at[c])
 
     def widened(ref, rs, cols):
         return dot(ref[rs, :], r.widen[:, cols])
@@ -355,18 +368,21 @@
             for copy in gathers[b + 1][2:4]:
                 copy.start()
 
+    def pair_here(b, k):
+        landing = r.xt.at[rows_of(b), place(k)]
+        remote("head", across, landing, landing, r.g_send.at[0], r.g_recv.at[4 * b + k + 1]).wait_recv()
+
     def direct_here(b):
-        gathers[b][2].wait_recv()
-        gathers[b][3].wait_recv()
+        pair_here(b, 1)
 
     def relayed_here(b):
-        gathers[b][4].wait_recv()
-        gathers[b][5].wait_recv()
+        pair_here(b, 2)
 
     for copy in loads[0]:
         copy.wait()
-    for b in range(blocks):
-        projected(b, 0, "xz")
+    for copy in loads[3]:
+        copy.start()
+    projected(0, 0, "xz")
     if cores == 2:
 
         @pl.when(core == 1)
@@ -375,20 +391,22 @@
             send_first()
 
     relay(0)
+    for b in range(1, blocks):
+        projected(b, 0, "xz")
     for k in (1, 2):
         for copy in loads[k]:
             copy.wait()
     for b in range(blocks):
         direct_here(b)
         projected(b, 1, "x")
+        if b + 1 < blocks:
+            relay(b + 1)
         if b == 0:
             projected(b, 1, "z")
             for copy in loads[3]:
                 copy.wait()
             for copy in out_loads:
                 copy.start()
-        if b + 1 < blocks:
-            relay(b + 1)
         relayed_here(b)
         late_small(b)
         prepare(b)
@@ -416,123 +434,160 @@
     def picked(low, high):
         return [c for k in range(low, high) for c in picks[k]]
 
-    late_count = pairs * 8 // 10
+    def both(one, two):
+        slot(1, picked(*one))
+        slot(2, picked(*two))
+
     late_z(0)
+    both((0, 1), (0, 0))
     for b in range(1, blocks):
-        projected(b, 1, "z")
-    slot(1, picked(0, 1))
+        projected(b, 1, "z", tiles[:some])
+        both((1, 3), (0, 0))
+        projected(b, 1, "z", tiles[some:])
+    both((3, 5), (0, 0))
     for b in range(1, blocks):
-        late_z(b)
-    slot(1, picked(1, 4))
-    passes = {0: ((4, 6), (0, 0)), 1: ((6, 10), (0, 2)), 2: ((0, 0), (2, 5)), 3: ((0, 0), (5, 8))}
+        late_z(b, tiles[:some])
+        both((5, 6), (0, 0))
+        late_z(b, tiles[some:])
+    both((6, 8), (0, 0))
+    turns = {0: ((8, 10), (0, 1)), 1: ((0, 0), (1, 3)), 2: ((0, 0), (3, 5)), 3: ((0, 0), (5, 8)), 4: ((0, 0), (8, 10)), 5: ((0, 0), (0, 0))}
+    turn = 0
     for i in range(chunks):
         if i % parts:
             middle(i)
+            both(*turns[turn])
+            turn += 1
         within(i)
-        for at in (1, 2):
-            slot(at, picked(*passes[i][at - 1]))
+        both(*turns[turn])
+        turn += 1
 
     r.sums[...] = jnp.zeros_like(r.sums)
 
-    def finish(c, _):
-        cols = pl.ds(pl.multiple_of(c * LANES, LANES), LANES)
-
-        @pl.when((pos > 2) | ((pos == 2) & (c >= late_count)) | ((pos > 0) & (pos == chain - 1)))
+    def finish(cols):
+        @pl.when((pos > 2) | ((pos > 0) & (pos == chain - 1)))
         def _():
-            down(c).wait_recv()
-
-            @pl.when(pos < chain - 1)
-            def _():
-                pass_on(c, cols)
-
-        carried = dot(r.mapped[:, NSTATE:], r.arrived[c])
+            for c in departures(cols):
+                down(c).wait_recv()
+
+                @pl.when(pos < chain - 1)
+                def _():
+                    pass_on(c, slice(c * LANES, (c + 1) * LANES))
+
+        arrived = jnp.concatenate([r.arrived[c] for c in departures(cols)], axis=1)
+        carried = dot(r.mapped[:, NSTATE:], arrived)
         gated = r.y[:, cols] + r.factor[:, cols] * carried
         r.g[:, cols] = (gated * r.gain[:, cols]).astype(BF16)
-        r.sums[...] = r.sums[...] + gated * gated
-        return 0
-
-    lax.fori_loop(0, pairs, finish, 0)
+        power = gated * gated
+        total_power = r.sums[...]
+        for k in range(0, cols.stop - cols.start, LANES):
+            total_power = total_power + power[:, k : k + LANES]
+        r.sums[...] = total_power
 
     for copy in out_loads:
         copy.wait()
+    upper_half, lower_half = slice(0, rows // 2), slice(rows // 2, rows)
+    ahead = tiles[-1].start
+    for cols in tiles[:-1]:
+        finish(cols)
+    for k, rs in enumerate((upper_half, lower_half)):
+        r.part[k] = dot(r.g[rs, :ahead], r.vw[0, :ahead, :])
+    finish(tiles[-1])
+
     small = [
-        remote("head", to, r.squares.at[k], r.others.at[k], r.q_send.at[k], r.q_recv.at[k])
+        remote("head", to, r.squares.at[k], r.others.at[k], r.q_send.at[0], r.q_recv.at[k])
         for k, to in enumerate((across, along))
     ]
+    pieces = rows // 2 // half
+
+    def place_of(p, k):
+        return 2 * p + k if k < 2 else 2 * pieces if k < 4 else 2 * pieces + 1 + p
+
     scatters = [
         [
-            remote("head", to, r.sent.at[6 * b + k], r.back.at[6 * b + k], r.o_send.at[6 * b + k], r.o_recv.at[6 * b + k])
+            remote("head", to, r.sent.at[pieces * k + p], r.back.at[pieces * k + p], r.o_send.at[0], r.o_recv.at[place_of(p, k)])
             for k, to in enumerate((across, along, across, along, along, across))
         ]
-        for b in range(blocks)
+        for p in range(pieces)
     ]
 
-    def put(b, k, value):
-        r.sent[6 * b + k] = value.astype(BF16)
-        scatters[b][k].start()
+    def put(p, k, value):
+        r.sent[pieces * k + p] = value.astype(BF16)
+        scatters[p][k].start()
+
+    def piece(p):
+        return slice(p * half, (p + 1) * half)
 
     def share(k, rs):
         return dot(r.g[rs, :], r.vw[k])
 
-    def direct(b):
-        lo, hi = slice(b * GROUP, b * GROUP + half), slice(b * GROUP + half, (b + 1) * GROUP)
-        put(b, 0, share(0, lo))
-        put(b, 1, share(0, hi))
-        put(b, 2, share(1, lo))
-        put(b, 3, share(2, hi))
-
-    def joined(b):
-        lo, hi = slice(b * GROUP, b * GROUP + half), slice(b * GROUP + half, (b + 1) * GROUP)
-        value = share(2, lo)
-        scatters[b][0].wait_recv()
-        put(b, 4, value + r.back[6 * b].astype(F32))
-        value = share(1, hi)
-        scatters[b][1].wait_recv()
-        put(b, 5, value + r.back[6 * b + 1].astype(F32))
-
-    slot = lax.broadcasted_iota(jnp.int32, (8, LANES), 0)
-    for b in range(blocks):
-        direct(b)
-        if b == 0:
-            squares = jnp.zeros((8, LANES), F32)
-            for i in range(chunks):
-                row = dot_nt(jnp.ones((8, LANES), F32), r.sums[chunk_rows(i), :], lax.Precision.HIGHEST)
-                squares = jnp.where(slot == i, row, squares)
-            r.squares[0] = squares
-            small[0].start()
-        if b:
-            joined(b - 1)
+    def direct(k, source, rs):
+        if source:
+            value = share(source, rs)
+        else:
+            value = r.part[k] + dot(r.g[rs, ahead:], r.vw[0, ahead:, :])
+        for p in range(pieces):
+            put(p, k, value[piece(p), :])
+
+    def joined(p):
+        for k in (0, 1):
+            scatters[p][k].wait_recv()
+            put(p, 4 + k, r.part[k, piece(p), :] + r.back[pieces * k + p].astype(F32))
+
+    direct(0, 0, upper_half)
+    direct(1, 0, lower_half)
+    spot = lax.broadcasted_iota(jnp.int32, (8, LANES), 0)
+    squares = jnp.zeros((8, LANES), F32)
+    for i in range(chunks):
+        row = dot_nt(jnp.ones((8, LANES), F32), r.sums[chunk_rows(i), :], lax.Precision.HIGHEST)
+        squares = jnp.where(spot == i, row, squares)
+    r.squares[0] = squares
+    small[0].start()
+    direct(2, 1, upper_half)
+    direct(3, 2, lower_half)
+    r.part[0] = share(2, upper_half)
+    r.part[1] = share(1, lower_half)
+    for p in range(pieces):
+        joined(p)
     small[0].wait_recv()
     r.squares[1] = r.squares[0] + r.others[0]
     small[1].start()
-    joined(blocks - 1)
     own = r.y
-    for b in range(blocks):
-        own[rows_of(b), :depth] = share(3, rows_of(b))
+    for rs in (upper_half, lower_half):
+        own[rs, :depth] = share(3, rs)
+    landing = r.back.at[2 * pieces : 4 * pieces]
+    remote("head", across, landing, landing, r.o_send.at[0], r.o_recv.at[2 * pieces]).wait_recv()
+    for k in (2, 3):
+        base = (k - 2) * (rows // 2)
+        for p in range(pieces):
+            span = slice(base + p * half, base + (p + 1) * half)
+            for i in range(depth // LANES):
+                cols = slice(i * LANES, (i + 1) * LANES)
+                own[span, cols] = own[span, cols] + r.back[pieces * k + p, :, cols].astype(F32)
     small[1].wait_recv()
     scale = lax.rsqrt((r.squares[1] + r.others[1]) / total + EPS)
     for i in range(chunks):
         r.sums[chunk_rows(i), :] = jnp.broadcast_to(scale[i : i + 1, :], (LANES, CHUNK)).T
-    for b in range(blocks):
-        for base, picks in ((b * GROUP, (2, 4)), (b * GROUP + half, (3, 5))):
-            span = slice(base, base + half)
-            for k in picks:
-                scatters[b][k].wait_recv()
+    for p in range(pieces):
+        landing = r.back.at[0:2]
+        remote("head", across, landing, landing, r.o_send.at[0], r.o_recv.at[2 * pieces + 1 + p]).wait_recv()
+        for k in (4, 5):
+            base = (k - 4) * (rows // 2)
+            span = slice(base + p * half, base + (p + 1) * half)
             for i in range(depth // LANES):
                 cols = slice(i * LANES, (i + 1) * LANES)
-                value = own[span, cols]
-                for k in picks:
-                    value = value + r.back[6 * b + k, :, cols].astype(F32)
+                value = own[span, cols] + r.back[pieces * k + p, :, cols].astype(F32)
                 out[span, cols] = (value * r.sums[span, :]).astype(BF16)
 
-    for group in gathers + scatters + [small]:
-        for copy in group:
-            copy.wait_send()
+    for ref, send, recv in (
+        (r.xt.at[:, : 3 * depth], r.g_send.at[0], r.g_recv.at[0]),
+        (r.sent, r.o_send.at[0], r.o_recv.at[0]),
+        (r.squares, r.q_send.at[0], r.q_recv.at[0]),
+    ):
+        remote("head", across, ref, ref, send, recv).wait_send()
 
     @pl.when(pos < chain - 1)
     def _():
-        for c in range(pairs):
-            down(c).wait_send()
+        remote("seq", upper, r.leaving, r.leaving, r.c_send.at[0], r.c_recv.at[0]).wait_send()
 
 
 def layer(chain, split, cores, tokens, resets, w_x, w_z, w_bc, w_dt, dt_bias, decay_rate, d_skip, norm_gain, w_out):
@@ -596,18 +651,18 @@
         sums=vm((rows, LANES), F32),
         squares=vm((2, 8, LANES), F32),
         others=vm((2, 8, LANES), F32),
-        sent=vm((6 * blocks, half, depth), BF16),
-        back=vm((6 * blocks, half, depth), BF16),
+        part=vm((2, rows // 2, depth), F32),
+        sent=vm((3 * rows // half, half, depth), BF16),
+        back=vm((3 * rows // half, half, depth), BF16),
         small_load=dma((7,)),
-        load=dma((12,)),
-        load_out=dma((4,)),
-        g_send=dma((6 * blocks,)),
-        g_recv=dma((6 * blocks,)),
-        c_send=dma((pairs,)),
+        load=dma((9,)),
+        g_send=dma((1,)),
+        g_recv=dma((4 * blocks,)),
+        c_send=dma((1,)),
         c_recv=dma((pairs,)),
-        o_send=dma((6 * blocks,)),
-        o_recv=dma((6 * blocks,)),
-        q_send=dma((2,)),
+        o_send=dma((1,)),
+        o_recv=dma((3 * rows // 2 // half + 1,)),
+        q_send=dma((1,)),
         q_recv=dma((2,)),
         go=pltpu.SemaphoreType.REGULAR((1,)),
     )

time: 59.1 us -> 55.9 us (0.946)
  the two profiles are of different devices: /device:TPU:25 before, /device:TPU:1 now
where the time goes in v3:
time: 55.9 us; the launch traced here: 55.7 us
  Pallas kernels  54.9 us (98%)
  local copies, waits for them, and re-layouts  0.84 us (2%)
    pallas_call x1, Pallas kernels, layer(): pl.pallas_call(functools.partial(kernel, chain, cores, float(width * spli...  54.9 us

profile of v3, /device:TPU:1, one launch (start us, length us, event | category | flops | bytes accessed | tf_op | source)
XLA Modules:
  0.0 55.7 jit_solution(16976968357579357767)
XLA Ops:
  0.0 54.9 %shard_map.109 = bf16[512,640]{1,0:T(8,128)(2,1)S(1)} custom-call(bf16[512,640]{1,0:T(8,128)(2,1)} %tok.1, s32[1,512]{1,0:T(1,128)} %bitcast.8, bf16[2560,1280]{1,0:T(8,128)(2,1)} %w_x.1, bf16[2560,1280]{1,0:T(8,128)(2,1)} %w_z.1, bf16[2560,256]{1,0:T(8,128)(2,1)} %w_bc.1, bf16[20,2560]{1,0:T(8,128)(2,1)} %bitcast.6, f32[1,20]{1,0:T(1,128)} %bitcast.9, ...), custom_call_target="tpu_custom_call" | custom-call | tf_op jit(solution)/shard_map/pallas_call | solution.py:669
  54.9 0.8 %copy.13 = bf16[512,640]{1,0:T(8,128)(2,1)} copy(bf16[512,640]{1,0:T(8,128)(2,1)S(1)} %shard_map.109) | data formatting | bytes 1310720

commit v4 on v3

--- a/solution.py
+++ b/solution.py
@@ -37,7 +37,8 @@
 
 
 def silu(v):
-    return v / (1.0 + jnp.exp(-v))
+    part = 0.5 * v
+    return part + part * jnp.tanh(part)
 
 
 class Scratch:
@@ -68,6 +69,7 @@
     width = w_x.shape[1]
     heads = w_dt.shape[0]
     core, other_core = lax.axis_index("batch"), 1 - lax.axis_index("batch")
+    leader = cores - 1
     blocks, pairs, per = rows // GROUP, width // LANES, LANES // HEADDIM
     half = GROUP // 2
     chunks, parts = rows // CHUNK, GROUP // CHUNK
@@ -160,7 +162,7 @@
             for copy in copies[:2]:
                 copy.start()
 
-    @pl.when(core == 0)
+    @pl.when(core == leader)
     def _():
         send_first()
 
@@ -385,7 +387,7 @@
     projected(0, 0, "xz")
     if cores == 2:
 
-        @pl.when(core == 1)
+        @pl.when(core != leader)
         def _():
             pl.semaphore_wait(r.go.at[0], 1)
             send_first()
@@ -412,7 +414,7 @@
         prepare(b)
         if b == 0 and cores == 2:
 
-            @pl.when(core == 0)
+            @pl.when(core == leader)
             def _():
                 pl.semaphore_signal(r.go.at[0], inc=1, device_id={"batch": other_core}, device_id_type=MESH)
 
@@ -422,12 +424,13 @@
             for cols in tiles:
                 block_state(b, cols)
         else:
-            late_x(b, tiles[0])
-            for k, cols in enumerate(tiles):
-                if k + 1 < len(tiles):
-                    late_x(b, tiles[k + 1])
-                block_state(b, cols)
-                leave_first(cols)
+            for low, high in ((0, 1), (1, 3), (3, len(tiles))):
+                group = tiles[low:high]
+                for cols in group:
+                    late_x(b, cols)
+                for cols in group:
+                    block_state(b, cols)
+                leave_first(slice(group[0].start, group[-1].stop))
 
     picks = [range(pairs * k // 10, pairs * (k + 1) // 10) for k in range(10)]
 

time: 55.9 us -> 54.4 us (0.973)
  the two profiles are of different devices: /device:TPU:1 before, /device:TPU:24 now
where the time goes in v4:
time: 54.4 us; the launch traced here: 53.5 us
  Pallas kernels  52.7 us (97%)
  local copies, waits for them, and re-layouts  0.84 us (2%)
    pallas_call x1, Pallas kernels, layer(): pl.pallas_call(functools.partial(kernel, chain, cores, float(width * spli...  52.7 us

profile of v4, /device:TPU:24, one launch (start us, length us, event | category | flops | bytes accessed | tf_op | source)
XLA Modules:
  0.0 53.5 jit_solution(13019268053654189875)
XLA Ops:
  0.0 52.7 %shard_map.109 = bf16[512,640]{1,0:T(8,128)(2,1)S(1)} custom-call(bf16[512,640]{1,0:T(8,128)(2,1)} %tok.1, s32[1,512]{1,0:T(1,128)} %bitcast.8, bf16[2560,1280]{1,0:T(8,128)(2,1)} %w_x.1, bf16[2560,1280]{1,0:T(8,128)(2,1)} %w_z.1, bf16[2560,256]{1,0:T(8,128)(2,1)} %w_bc.1, bf16[20,2560]{1,0:T(8,128)(2,1)} %bitcast.6, f32[1,20]{1,0:T(1,128)} %bitcast.9, ...), custom_call_target="tpu_custom_call" | custom-call | tf_op jit(solution)/shard_map/pallas_call | solution.py:672
  52.7 0.8 %copy.13 = bf16[512,640]{1,0:T(8,128)(2,1)} copy(bf16[512,640]{1,0:T(8,128)(2,1)S(1)} %shard_map.109) | data formatting | bytes 1310720

commit v5 on v4

--- a/solution.py
+++ b/solution.py
@@ -410,14 +410,14 @@
             for copy in out_loads:
                 copy.start()
         relayed_here(b)
-        late_small(b)
-        prepare(b)
         if b == 0 and cores == 2:
 
             @pl.when(core == leader)
             def _():
                 pl.semaphore_signal(r.go.at[0], inc=1, device_id={"batch": other_core}, device_id_type=MESH)
 
+        late_small(b)
+        prepare(b)
         if b + 1 < blocks:
             for cols in tiles:
                 late_x(b, cols)

time: 54.4 us -> 55.2 us (1.015)
  the two profiles are of different devices: /device:TPU:24 before, /device:TPU:0 now
where the time goes in v5:
time: 55.2 us; the launch traced here: 55 us
  Pallas kernels  54.2 us (98%)
  local copies, waits for them, and re-layouts  0.84 us (2%)
    pallas_call x1, Pallas kernels, layer(): pl.pallas_call(functools.partial(kernel, chain, cores, float(width * spli...  54.2 us

profile of v5, /device:TPU:0, one launch (start us, length us, event | category | flops | bytes accessed | tf_op | source)
XLA Modules:
  0.0 55.0 jit_solution(15728170627157026162)
XLA Ops:
  0.0 54.2 %shard_map.109 = bf16[512,640]{1,0:T(8,128)(2,1)S(1)} custom-call(bf16[512,640]{1,0:T(8,128)(2,1)} %tok.1, s32[1,512]{1,0:T(1,128)} %bitcast.8, bf16[2560,1280]{1,0:T(8,128)(2,1)} %w_x.1, bf16[2560,1280]{1,0:T(8,128)(2,1)} %w_z.1, bf16[2560,256]{1,0:T(8,128)(2,1)} %w_bc.1, bf16[20,2560]{1,0:T(8,128)(2,1)} %bitcast.6, f32[1,20]{1,0:T(1,128)} %bitcast.9, ...), custom_call_target="tpu_custom_call" | custom-call | tf_op jit(solution)/shard_map/pallas_call | solution.py:672
  54.2 0.8 %copy.13 = bf16[512,640]{1,0:T(8,128)(2,1)} copy(bf16[512,640]{1,0:T(8,128)(2,1)S(1)} %shard_map.109) | data formatting | bytes 1310720
